TPU v7x, 32 devices: a whole 2x2x4 slice. The times are simulated.
32 devices in a mesh: expert: 16 (over z, y, x), tensor: 2 (over core).
Axes of the slice: x: 2, y: 2, z: 4, core: 2. Of those that a mesh axis runs over, the one named last changes fastest.
Arguments:
- grad_out: bfloat16 [256, 3584], P('expert'), may hold values from -1.5 to 1.5
- expert_ids: int32 [256, 8], P('expert'), may hold values from 0 to 15, all different within a row; in each aligned block of 16 rows (0 to 15, 16 to 31, ...) at most 16 rows name the same one
- gate_values: float32 [256, 8], P('expert'), may hold values from 0.05 to 0.6
- w_gate_up: bfloat16 [16, 2, 3584, 1024], P('expert', None, None, 'tensor'), may hold values from -0.09375 to 0.09375
- w_down: bfloat16 [16, 1024, 3584], P('expert', 'tensor'), may hold values from -0.1875 to 0.1875
- saved_routed: bfloat16 [16, 2, 256, 1024], P('expert', None, None, 'tensor'), may hold values from -6 to 6
- shared_gate_up: bfloat16 [2, 3584, 1024], P(None, 'expert', 'tensor'), may hold values from -0.09375 to 0.09375
- shared_down: bfloat16 [1024, 3584], P('tensor', 'expert'), may hold values from -0.1875 to 0.1875
- saved_shared: bfloat16 [2, 256, 1024], P(None, 'expert', 'tensor'), may hold values from -6 to 6
Outputs:
- grad_in: bfloat16 [256, 3584], P('expert', 'tensor')
- grad_gates: float32 [256, 8], P('expert')
Inputs may be any that keep to these rules, and one draw needn't show every extreme that they name: `expert_ids`: each row names 8 different experts. Among the 16 rows of one index of expert (aligned blocks of rows), no expert is named by more than 16 rows, and in some block one expert is named by exactly 16 rows.
All inputs are finite; a program needn't handle non-finite values.
Results may differ from a plain program's by a relative error of at most 0.015.
Values may be sent and summed in bfloat16 or wider, within the bound.
A program may use at most 64 MiB of HBM per device.

v0:
```python
import jax
import jax.numpy as jnp
from jax import lax
from jax.sharding import PartitionSpec as P


def contract_last(left_side, right_side):
    return lax.dot_general(
        left_side, right_side, (((1,), (1,)), ((), ())), preferred_element_type=jnp.float32
    )


def swiglu_grads(back_grad, saved_gate, saved_up):
    pre_gate = saved_gate.astype(jnp.float32)
    pre_up = saved_up.astype(jnp.float32)
    sigmoid = jax.nn.sigmoid(pre_gate)
    grad_gate = (back_grad * pre_up * sigmoid * (1.0 + pre_gate * (1.0 - sigmoid))).astype(
        jnp.bfloat16
    )
    grad_up = (back_grad * pre_gate * sigmoid).astype(jnp.bfloat16)
    return (grad_gate, grad_up)


def gate_mixture(back_grad, saved_gate, saved_up):
    pre_gate = saved_gate.astype(jnp.float32)
    pre_up = saved_up.astype(jnp.float32)
    sigmoid = jax.nn.sigmoid(pre_gate)
    return back_grad * pre_gate * sigmoid * pre_up


def per_device(
    grad_out,
    expert_ids,
    gate_values,
    w_gate_up,
    w_down,
    saved_routed,
    shared_gate_up,
    shared_down,
    saved_shared,
):
    experts = lax.axis_size("expert")
    tokens, features = grad_out.shape
    choose = expert_ids.shape[1]
    slot_count = saved_routed.shape[2]
    capacity = slot_count // experts
    flat_ids = expert_ids.reshape(-1)
    onehot = (flat_ids[:, None] == jnp.arange(experts, dtype=jnp.int32)[None, :]).astype(jnp.int32)
    earlier = jnp.cumsum(onehot, axis=0) - onehot
    position = jnp.sum(earlier * onehot, axis=1)
    slot_index = flat_ids * capacity + position
    pair_token = jnp.arange(tokens * choose, dtype=jnp.int32) // choose
    source_row = jnp.full((slot_count,), tokens, jnp.int32).at[slot_index].set(pair_token)
    padded = jnp.concatenate([grad_out, jnp.zeros((1, features), grad_out.dtype)], axis=0)
    send_rows = padded[source_row].reshape(experts, capacity, features)
    arrived = lax.all_to_all(send_rows, "expert", split_axis=0, concat_axis=0, tiled=True)
    slot_rows = arrived.reshape(slot_count, features)
    back_grad = contract_last(slot_rows, w_down[0])
    grad_gate, grad_up = swiglu_grads(back_grad, saved_routed[0, 0], saved_routed[0, 1])
    gate_mix = gate_mixture(back_grad, saved_routed[0, 0], saved_routed[0, 1])
    row_terms = contract_last(grad_gate, w_gate_up[0, 0]) + contract_last(grad_up, w_gate_up[0, 1])
    gate_terms = jnp.sum(gate_mix, axis=1).astype(jnp.bfloat16)
    shared_back = contract_last(grad_out, lax.all_gather(shared_down, "expert", axis=1, tiled=True))
    shared_gate, shared_up = swiglu_grads(shared_back, saved_shared[0], saved_shared[1])
    weight_piece = lax.all_gather(shared_gate_up, "expert", axis=1, tiled=True)
    shared_term = contract_last(shared_gate, weight_piece[0]) + contract_last(
        shared_up, weight_piece[1]
    )
    outgoing = row_terms.astype(jnp.bfloat16).reshape(experts, capacity, features)
    returned, gate_back = (
        lax.all_to_all(outgoing, "expert", split_axis=0, concat_axis=0, tiled=True),
        lax.all_to_all(
            gate_terms.reshape(experts, capacity), "expert", split_axis=0, concat_axis=0, tiled=True
        ),
    )
    picked = returned.reshape(slot_count, features)[slot_index].reshape(tokens, choose, features)
    routed = jnp.einsum("tkd,tk->td", picked.astype(jnp.float32), gate_values)
    summed = lax.psum_scatter(
        (routed + shared_term).astype(jnp.bfloat16), "tensor", scatter_dimension=1, tiled=True
    )
    gate_pairs = (
        gate_back.reshape(slot_count)[slot_index].reshape(tokens, choose).astype(jnp.float32)
    )
    grad_gates = lax.psum(gate_pairs, "tensor")
    return (summed, grad_gates)


def solution(mesh):
    return jax.shard_map(
        per_device,
        mesh=mesh,
        in_specs=(
            P("expert", None),
            P("expert", None),
            P("expert", None),
            P("expert", None, None, "tensor"),
            P("expert", "tensor", None),
            P("expert", None, None, "tensor"),
            P(None, "expert", "tensor"),
            P("tensor", "expert"),
            P(None, "expert", "tensor"),
        ),
        out_specs=(P("expert", "tensor"), P("expert", None)),
        check_vma=False,
    )
```

profile of v0, /device:TPU:0, one launch (start us, length us, event | category | flops | bytes accessed | tf_op | source)
XLA Modules:
  0.0 253.5 jit_solution(2283505379111606184)
XLA Ops:
  7.2 0.7 all-gather.3.cloned.1.call-update
  7.9 0.7 all-gather.5.cloned.1.call-update
  8.6 0.8 copy.18
  9.4 0.1 eq.15
  9.5 0.7 broadcast_multiply_fusion
  10.3 0.1 mul.62
  10.4 0.1 fusion.29
  10.4 0.2 reduce_window_sum.11
  10.6 0.9 concatenate.3
  11.5 0.2 select_reduce_fusion
  11.7 1.0 scatter_custom_fusion
  12.8 1.7 gather_fusion
  14.5 66.9 %all_to_all.16 = bf16[16,16,3584]{2,1,0:T(8,128)(2,1)S(1)} all-to-all(bf16[16,16,3584]{2,1,0:T(8,128)(2,1)S(1)} %bitcast.73), channel_id=1, replica_groups=mesh['expert'=16,'tensor'=2] {'expert'}, dimensions={0} | all-to-all | bytes 3670016 | tf_op jit(solution)/shard_map/all_to_all | solution.py:56
  81.4 1.3 fusion.16
  82.7 3.4 %fusion.5 = f32[256,3584]{1,0:T(8,128)S(1)} fusion(bf16[1,2,3584,512]{3,2,1,0:T(8,128)(2,1)} %param.12, f32[256,512]{1,0:T(8,128)S(1)} %get-tuple-element.9, bf16[1,2,256,512]{3,2,1,0:T(8,128)(2,1)S(1)} %copy-done.4), kind=kOutput, calls=%fused_computation.13 | convolution fusion | flops 941096960 | bytes 8388608 | tf_op jit(solution)/shard_map/dot_general | solution.py:8
  86.2 2.4 fusion
  88.6 7.1 %all-to-all-start.1 = ((bf16[16,16,3584]{2,1,0:T(8,128)(2,1)}), bf16[16,16,3584]{2,1,0:T(8,128)(2,1)S(1)}, u32[]{:S(2)}, u32[]{:S(2)}) async-start(bf16[16,16,3584]{2,1,0:T(8,128)(2,1)} %bitcast.74), calls=%async_computation.1 | async-start | bytes 3670016 | tf_op jit(solution)/shard_map/all_to_all | solution.py:71
  95.8 0.1 copy.21
  95.9 47.3 %all-to-all-done.1 = bf16[16,16,3584]{2,1,0:T(8,128)(2,1)S(1)} async-done(((bf16[16,16,3584]{2,1,0:T(8,128)(2,1)}), bf16[16,16,3584]{2,1,0:T(8,128)(2,1)S(1)}, u32[]{:S(2)}, u32[]{:S(2)}) %all-to-all-start.1) | async-done | bytes 1835040 | tf_op jit(solution)/shard_map/all_to_all | solution.py:71
  143.2 1.1 gather_fusion.1
  144.4 0.4 fusion.11
  144.8 2.6 %fusion.56 = f32[16,512]{1,0:T(8,128)S(1)} fusion(bf16[16,3584]{1,0:T(8,128)(2,1)S(1)} %copy-done, bf16[512,3584]{0,1:T(8,128)(2,1)} %all-gather.3.cloned.1.call-done), kind=kOutput, calls=%fused_computation.81 | convolution fusion | flops 58720256 | bytes 3817472 | tf_op jit(solution)/shard_map/dot_general | solution.py:8
  147.4 76.9 %all-gather.5.cloned.1.call-done = bf16[2,3584,512]{2,1,0:T(8,128)(2,1)} async-done(((bf16[2,224,512]{2,1,0:T(8,128)(2,1)}), bf16[2,3584,512]{2,1,0:T(8,128)(2,1)}) %all-gather.5.cloned.1.call-update) | async-done | bytes 7340048 | tf_op jit(solution)/shard_map/all_gather | solution.py:65
  224.3 3.1 %fusion.3 = f32[16,3584]{1,0:T(8,128)S(1)} fusion(bf16[2,3584,512]{2,1,0:T(8,128)(2,1)} %all-gather.5.cloned.1.call-done, f32[16,512]{1,0:T(8,128)S(1)} %fusion.56, bf16[2,16,512]{2,1,0:T(8,128)(2,1)S(1)} %copy-done.1), kind=kOutput, calls=%fused_computation.11 | convolution fusion | flops 58818560 | bytes 3964928 | tf_op jit(solution)/shard_map/dot_general | solution.py:8
  227.4 3.8 %fusion.2 = bf16[16,3584]{1,0:T(8,128)(2,1)} fusion(f32[16,3584]{1,0:T(8,128)S(1)} %fusion.3, bf16[2,3584,512]{2,1,0:T(8,128)(2,1)} %all-gather.5.cloned.1.call-done, f32[16,1,3584]{2,1,0:T(1,128)S(1)} %fusion.11, f32[16,512]{1,0:T(8,128)S(1)} %fusion.56, bf16[2,16,512]{2,1,0:T(8,128)(2,1)S(1)} %copy-done.1), kind=kOutput, calls=%fused_computation.8 | convolution fusion | flops 58949632 | bytes 4292608 | tf_op jit(solution)/shard_map/dot_general | solution.py:8
  231.2 0.1 convert_element_type.92
  231.3 11.1 %all_to_all.17 = bf16[16,1,16]{2,1,0:T(2,128)(2,1)S(1)} all-to-all(bf16[16,1,16]{2,1,0:T(2,128)(2,1)S(1)} %convert_element_type.92), channel_id=1, replica_groups=mesh['expert'=16,'tensor'=2] {'expert'}, dimensions={0} | all-to-all | bytes 1024 | tf_op jit(solution)/shard_map/all_to_all | solution.py:72
  242.4 0.1 reshape.84
  242.5 1.2 gather_fusion.2
  243.7 0.1 reshape.89
  243.8 2.5 psum.7
  246.3 0.7 copy.20
  (28 shorter events, 0.3 us)
Async XLA Ops:
  7.2 137.6 %all-gather.3.cloned.1.call-start = ((), (), s32[]{:S(2)}) async-start(), calls=%async_computation.4 | async-start | bytes 3899392 | tf_op jit(solution)/shard_map/all_gather | solution.py:63
  7.9 216.4 %all-gather.5.cloned.1.call-start = ((), (), s32[]{:S(2)}) async-start(), calls=%async_computation.5 | async-start | bytes 7798784 | tf_op jit(solution)/shard_map/all_gather | solution.py:65
  12.7 68.7 %copy-start.4 = (bf16[1,2,256,512]{3,2,1,0:T(8,128)(2,1)S(1)}, bf16[1,2,256,512]{3,2,1,0:T(8,128)(2,1)}, u32[]{:S(2)}) copy-start(bf16[1,2,256,512]{3,2,1,0:T(8,128)(2,1)} %param.14) | copy-start | bytes 1572868
  14.5 66.9 %copy-start.3 = (bf16[1,512,3584]{2,1,0:T(8,128)(2,1)S(1)}, bf16[1,512,3584]{2,1,0:T(8,128)(2,1)}, u32[]{:S(2)}) copy-start(bf16[1,512,3584]{2,1,0:T(8,128)(2,1)} %param.13) | copy-start | bytes 11010052
  81.4 4.8 %slice-start = ((s8[7340032]{0:T(1024)(128)(4,1)}), s8[4194304]{0:T(1024)(128)(4,1)S(1)}, s32[]{:S(2)}) async-start(s8[7340032]{0:T(1024)(128)(4,1)} %bitcast.77), calls=%async_computation.7 | async-start | bytes 8388608
  82.7 3.5 %slice-start.1 = ((s8[7340032]{0:T(1024)(128)(4,1)}), s8[3145728]{0:T(1024)(128)(4,1)S(1)}, s32[]{:S(2)}) async-start(s8[7340032]{0:T(1024)(128)(4,1)} %bitcast.77), calls=%async_computation.8 | async-start | bytes 6291456
  88.6 7.2 %copy-start.2 = (f32[16,8]{0,1:T(8,128)S(1)}, f32[16,8]{0,1:T(8,128)}, u32[]{:S(2)}) copy-start(f32[16,8]{0,1:T(8,128)} %param.11) | copy-start | bytes 1540
  88.6 54.6 %all-to-all-start.1 = ((bf16[16,16,3584]{2,1,0:T(8,128)(2,1)}), bf16[16,16,3584]{2,1,0:T(8,128)(2,1)S(1)}, u32[]{:S(2)}, u32[]{:S(2)}) async-start(bf16[16,16,3584]{2,1,0:T(8,128)(2,1)} %bitcast.74), calls=%async_computation.1 | async-start | bytes 3670016 | tf_op jit(solution)/shard_map/all_to_all | solution.py:71
  95.8 151.2 %reduce-scatter.2.cloned.1.call-start = ((), (), s32[]{:S(2)}) async-start(), calls=%async_computation.6 | async-start | bytes 172032 | tf_op jit(solution)/shard_map/reduce_scatter | solution.py:78
  143.2 1.6 copy-start
  144.4 79.9 %copy-start.1 = (bf16[2,16,512]{2,1,0:T(8,128)(2,1)S(1)}, bf16[2,16,512]{2,1,0:T(8,128)(2,1)}, u32[]{:S(2)}) copy-start(bf16[2,16,512]{2,1,0:T(8,128)(2,1)} %param.17) | copy-start | bytes 98308
Sparse Core Ops, SparseCore 0:
  10.7 103.8 all-gather.2
  117.3 106.9 all-gather.4
  231.3 5.9 reduce-scatter.1
where the time goes:
time: 254 us; the launch traced here: 253 us
  waiting for transfers between devices  126 us (50%)
  blocking collectives  80.5 us (32%)
  matrix products  17 us (7%)
  between operations  13.9 us (5%)
  local copies, waits for them, and re-layouts  8 us (3%)
  starting transfers between devices  7.26 us (3%)
    all_gather x1, waiting for transfers between devices, per_device(): weight_piece = lax.all_gather(shared_gate_up, 'expert', axis=1, tiled=True)  76.9 us
    all_to_all x1, blocking collectives, per_device(): lax.all_to_all(send_rows, 'expert', split_axis=0, concat_axis=0, tiled=True)  66.9 us
    all_to_all x1, waiting for transfers between devices, per_device(): lax.all_to_all(outgoing, 'expert', split_axis=0, concat_axis=0, tiled=True)  47.3 us
    dot_general x6, matrix products, contract_last(): lax.dot_general(left_side, right_side, (((1,), (1,)), ((), ())), preferre...  16.7 us
    all_to_all x1, blocking collectives, per_device(): lax.all_to_all(gate_terms.reshape(experts, capacity), 'expert', split_axi...  11.1 us
    all_to_all x1, starting transfers between devices, per_device(): lax.all_to_all(outgoing, 'expert', split_axis=0, concat_axis=0, tiled=True)  7.14 us
  transfers between devices with their start and end apart: 4, of which 2 were waited for; matrix products, arithmetic and copies ran while one was open for 8% of the time, Pallas kernels for 0%

commit v1 on v0

--- a/solution.py
+++ b/solution.py
@@ -62,7 +62,7 @@
     gate_terms = jnp.sum(gate_mix, axis=1).astype(jnp.bfloat16)
     shared_back = contract_last(grad_out, lax.all_gather(shared_down, "expert", axis=1, tiled=True))
     shared_gate, shared_up = swiglu_grads(shared_back, saved_shared[0], saved_shared[1])
-    weight_piece = lax.all_gather(shared_gate_up, "expert", axis=1, tiled=True)
+    weight_piece = jnp.concatenate(lax.all_gather(shared_gate_up, "expert"), axis=1)
     shared_term = contract_last(shared_gate, weight_piece[0]) + contract_last(
         shared_up, weight_piece[1]
     )

time: 254 us -> 254 us (level)
  matrix products: 17 us -> 12.9 us
  local copies, waits for them, and re-layouts: 8 us -> 12 us
    dot_general x6, matrix products: 16.7 us -> 12.6 us  [contract_last(): lax.dot_general(left_side, right_side, (((1,), (1,)), ((), ())), preferre...]
    slice x0 -> x1, local copies, waits for them, and re-layouts: none -> 3.96 us  [per_device(): weight_piece[1]]
where the time goes in v1:
time: 254 us; the launch traced here: 253 us
  waiting for transfers between devices  126 us (50%)
  blocking collectives  80.4 us (32%)
  between operations  13.9 us (5%)
  matrix products  12.9 us (5%)
  local copies, waits for them, and re-layouts  12 us (5%)
  starting transfers between devices  7.26 us (3%)
    all_gather x1, waiting for transfers between devices, per_device(): lax.all_gather(shared_gate_up, 'expert')  76.8 us
    all_to_all x1, blocking collectives, per_device(): lax.all_to_all(send_rows, 'expert', split_axis=0, concat_axis=0, tiled=True)  66.9 us
    all_to_all x1, waiting for transfers between devices, per_device(): lax.all_to_all(outgoing, 'expert', split_axis=0, concat_axis=0, tiled=True)  47.4 us
    dot_general x6, matrix products, contract_last(): lax.dot_general(left_side, right_side, (((1,), (1,)), ((), ())), preferre...  12.6 us
    all_to_all x1, blocking collectives, per_device(): lax.all_to_all(gate_terms.reshape(experts, capacity), 'expert', split_axi...  11 us
    all_to_all x1, starting transfers between devices, per_device(): lax.all_to_all(outgoing, 'expert', split_axis=0, concat_axis=0, tiled=True)  7.14 us
  transfers between devices with their start and end apart: 4, of which 2 were waited for; matrix products, arithmetic and copies ran while one was open for 8% of the time, Pallas kernels for 0%

profile of v1, /device:TPU:0, one launch (start us, length us, event | category | flops | bytes accessed | tf_op | source)
XLA Modules:
  0.0 253.4 jit_solution(10387775928016344583)
XLA Ops:
  7.2 0.7 all-gather.4.cloned.1.call-update
  7.9 0.7 all-gather.6.cloned.1.call-update
  8.6 0.8 copy.18
  9.4 0.7 broadcast_multiply_fusion
  10.2 0.1 mul.62
  10.3 0.1 eq.15
  10.3 0.1 fusion.28
  10.4 0.2 reduce_window_sum.11
  10.6 0.9 concatenate.3
  11.5 0.2 select_reduce_fusion
  11.7 1.0 scatter_custom_fusion
  12.8 1.7 gather_fusion
  14.5 66.9 %all_to_all.16 = bf16[16,16,3584]{2,1,0:T(8,128)(2,1)S(1)} all-to-all(bf16[16,16,3584]{2,1,0:T(8,128)(2,1)S(1)} %bitcast.77), channel_id=1, replica_groups=mesh['expert'=16,'tensor'=2] {'expert'}, dimensions={0} | all-to-all | bytes 3670016 | tf_op jit(solution)/shard_map/all_to_all | solution.py:56
  81.4 1.3 fusion.15
  82.7 3.4 %fusion.4 = f32[256,3584]{1,0:T(8,128)S(1)} fusion(bf16[1,2,3584,512]{3,2,1,0:T(8,128)(2,1)} %param.12, f32[256,512]{1,0:T(8,128)S(1)} %get-tuple-element.11, bf16[1,2,256,512]{3,2,1,0:T(8,128)(2,1)S(1)} %copy-done.4), kind=kOutput, calls=%fused_computation.10 | convolution fusion | flops 941096960 | bytes 8388608 | tf_op jit(solution)/shard_map/dot_general | solution.py:8
  86.2 2.4 fusion
  88.6 7.1 %all-to-all-start.1 = ((bf16[16,16,3584]{2,1,0:T(8,128)(2,1)}), bf16[16,16,3584]{2,1,0:T(8,128)(2,1)S(1)}, u32[]{:S(2)}, u32[]{:S(2)}) async-start(bf16[16,16,3584]{2,1,0:T(8,128)(2,1)} %bitcast.79), calls=%async_computation.1 | async-start | bytes 3670016 | tf_op jit(solution)/shard_map/all_to_all | solution.py:71
  95.9 47.4 %all-to-all-done.1 = bf16[16,16,3584]{2,1,0:T(8,128)(2,1)S(1)} async-done(((bf16[16,16,3584]{2,1,0:T(8,128)(2,1)}), bf16[16,16,3584]{2,1,0:T(8,128)(2,1)S(1)}, u32[]{:S(2)}, u32[]{:S(2)}) %all-to-all-start.1) | async-done | bytes 1835040 | tf_op jit(solution)/shard_map/all_to_all | solution.py:71
  143.3 1.1 gather_fusion.1
  144.5 0.4 fusion.10
  144.9 2.6 %fusion.57 = f32[16,512]{1,0:T(8,128)S(1)} fusion(bf16[16,3584]{1,0:T(8,128)(2,1)S(1)} %copy-done, bf16[512,3584]{0,1:T(8,128)(2,1)} %all-gather.4.cloned.1.call-done), kind=kOutput, calls=%fused_computation.80 | convolution fusion | flops 58720256 | bytes 3817472 | tf_op jit(solution)/shard_map/dot_general | solution.py:8
  147.5 76.8 %all-gather.6.cloned.1.call-done = bf16[32,224,512]{2,1,0:T(8,128)(2,1)} async-done(((bf16[2,224,512]{2,1,0:T(8,128)(2,1)}), bf16[32,224,512]{2,1,0:T(8,128)(2,1)}) %all-gather.6.cloned.1.call-update) | async-done | bytes 7340048 | tf_op jit(solution)/shard_map/all_gather | solution.py:65
  224.3 4.0 %fusion.56 = (bf16[1,16,224,512]{3,2,0,1:T(8,128)(2,1)S(1)}, bf16[1,16,224,512]{3,2,0,1:T(8,128)(2,1)S(1)}) fusion(bf16[2,16,224,512]{3,2,0,1:T(8,128)(2,1)} %bitcast.78), kind=kLoop, calls=%fused_computation.79 | loop fusion | bytes 14680064 | tf_op jit(solution)/shard_map/slice | solution.py:67
  228.3 1.1 fusion.39
  229.4 1.7 fusion.2
  231.1 0.1 convert_element_type.92
  231.2 11.0 %all_to_all.17 = bf16[16,1,16]{2,1,0:T(2,128)(2,1)S(1)} all-to-all(bf16[16,1,16]{2,1,0:T(2,128)(2,1)S(1)} %convert_element_type.92), channel_id=1, replica_groups=mesh['expert'=16,'tensor'=2] {'expert'}, dimensions={0} | all-to-all | bytes 1024 | tf_op jit(solution)/shard_map/all_to_all | solution.py:72
  242.3 0.1 reshape.93
  242.4 1.2 gather_fusion.2
  243.6 0.1 reshape.98
  243.7 2.5 psum.7
  246.2 0.7 copy.20
  (29 shorter events, 0.4 us)
Async XLA Ops:
  7.2 137.7 %all-gather.4.cloned.1.call-start = ((), (), s32[]{:S(2)}) async-start(), calls=%async_computation.4 | async-start | bytes 3899392 | tf_op jit(solution)/shard_map/all_gather | solution.py:63
  7.9 216.4 %all-gather.6.cloned.1.call-start = ((), (), s32[]{:S(2)}) async-start(), calls=%async_computation.6 | async-start | bytes 7798784 | tf_op jit(solution)/shard_map/all_gather | solution.py:65
  12.7 68.7 %copy-start.4 = (bf16[1,2,256,512]{3,2,1,0:T(8,128)(2,1)S(1)}, bf16[1,2,256,512]{3,2,1,0:T(8,128)(2,1)}, u32[]{:S(2)}) copy-start(bf16[1,2,256,512]{3,2,1,0:T(8,128)(2,1)} %param.14) | copy-start | bytes 1572868
  14.5 66.9 %copy-start.3 = (bf16[1,512,3584]{2,1,0:T(8,128)(2,1)S(1)}, bf16[1,512,3584]{2,1,0:T(8,128)(2,1)}, u32[]{:S(2)}) copy-start(bf16[1,512,3584]{2,1,0:T(8,128)(2,1)} %param.13) | copy-start | bytes 11010052
  81.4 4.8 %slice-start = ((s8[7340032]{0:T(1024)(128)(4,1)}), s8[4194304]{0:T(1024)(128)(4,1)S(1)}, s32[]{:S(2)}) async-start(s8[7340032]{0:T(1024)(128)(4,1)} %bitcast.82), calls=%async_computation.7 | async-start | bytes 8388608
  82.7 3.5 %slice-start.1 = ((s8[7340032]{0:T(1024)(128)(4,1)}), s8[3145728]{0:T(1024)(128)(4,1)S(1)}, s32[]{:S(2)}) async-start(s8[7340032]{0:T(1024)(128)(4,1)} %bitcast.82), calls=%async_computation.8 | async-start | bytes 6291456
  88.6 7.2 %copy-start.2 = (f32[16,8]{0,1:T(8,128)S(1)}, f32[16,8]{0,1:T(8,128)}, u32[]{:S(2)}) copy-start(f32[16,8]{0,1:T(8,128)} %param.11) | copy-start | bytes 1540
  88.6 54.7 %all-to-all-start.1 = ((bf16[16,16,3584]{2,1,0:T(8,128)(2,1)}), bf16[16,16,3584]{2,1,0:T(8,128)(2,1)S(1)}, u32[]{:S(2)}, u32[]{:S(2)}) async-start(bf16[16,16,3584]{2,1,0:T(8,128)(2,1)} %bitcast.79), calls=%async_computation.1 | async-start | bytes 3670016 | tf_op jit(solution)/shard_map/all_to_all | solution.py:71
  95.8 151.1 %reduce-scatter.2.cloned.1.call-start = ((), (), s32[]{:S(2)}) async-start(), calls=%async_computation.5 | async-start | bytes 172032 | tf_op jit(solution)/shard_map/reduce_scatter | solution.py:78
  143.3 1.5 copy-start
  224.3 4.0 %copy-start.1 = (bf16[2,16,512]{2,1,0:T(8,128)(2,1)S(1)}, bf16[2,16,512]{2,1,0:T(8,128)(2,1)}, u32[]{:S(2)}) copy-start(bf16[2,16,512]{2,1,0:T(8,128)(2,1)} %param.17) | copy-start | bytes 98308
Sparse Core Ops, SparseCore 0:
  10.7 103.8 all-gather.3
  117.3 107.0 all-gather.5
  231.2 5.8 reduce-scatter.1
